TPU v7x, 256 devices: a 8x8x2 block of a 8x8x16 slice. The times are simulated.
256 devices in a mesh: tenant: 2 (over z), row: 128 (over x, y, core).
Axes of the slice: x: 8, y: 8, z: 2, core: 2. Of those that a mesh axis runs over, the one named last changes fastest.
The devices are a block of a 8x8x16 slice.
Arguments:
- queries: bfloat16 [32768, 256], P(('tenant', 'row')), parts along dimension 0, may hold values from -6 to 6
- probes: int32 [32768, 16], P(('tenant', 'row')), parts along dimension 0, may hold values from 0 to 1039, all different within a row; in each aligned block of 128 rows (0 to 127, 128 to 255, ...) at most 4 rows name the same one
- hot_lists: bfloat16 [32, 256, 256], P('tenant'), parts along dimension 0, may hold values from -0.375 to 0.375
- cold_lists: bfloat16 [2048, 256, 256], P(('tenant', 'row')), parts along dimension 0, may hold values from -0.375 to 0.375
Outputs:
- nearest: float32 [32768, 128], P(('tenant', 'row')), parts along dimension 0
There are 2 independent parts, one for each index of `tenant`. A program takes and returns all parts, laid end to end along the dimension named above; each array names one. Nothing has to cross between parts.
Inputs may be any that keep to these rules, and one draw needn't show every extreme that they name: `probes`: each query names 16 different lists; every list is named by some query. Within the queries of one index of row (aligned blocks of 128 rows) no list is named more than 4 times, a bound that some block reaches.
All inputs are finite; a program needn't handle non-finite values.
Results may differ from a plain program's by a relative error of at most 0.0003.
Values may be sent and summed in bfloat16 or wider, within the bound.
A program may use at most 64 MiB of HBM per device.

v0:
```python
import math

import jax
import jax.numpy as jnp
from jax import lax
from jax.sharding import PartitionSpec as P

TOPK = 128


def hot_scores(queries, hot_lists):
    hot_count, lsize, width = hot_lists.shape
    qcount = queries.shape[0]
    flat_hot = hot_lists.reshape(hot_count * lsize, width)
    scores = lax.dot_general(
        queries, flat_hot, (((1,), (1,)), ((), ())), preferred_element_type=jnp.float32
    )
    return scores.reshape(qcount, hot_count, lsize)


def earlier_equal(flat):
    count = flat.shape[0]
    block = math.gcd(count, 512)
    index_all = jnp.arange(count, dtype=jnp.int32)

    def one_block(start):
        ids = lax.dynamic_slice_in_dim(flat, start, block, 0)
        where_at = start + jnp.arange(block, dtype=jnp.int32)
        same = (ids[:, None] == flat[None, :]) & (index_all[None, :] < where_at[:, None])
        return jnp.sum(same.astype(jnp.int32), axis=1)

    starts = jnp.arange(count // block, dtype=jnp.int32) * block
    return lax.map(one_block, starts).reshape(count)


def shards(queries, probes, hot_lists, cold_lists):
    rows = lax.axis_size("row")
    qcount, nprobe = probes.shape
    list_dev = cold_lists.shape[0]
    hot_count, lsize, width = hot_lists.shape
    capacity = 2 * ((qcount * nprobe + list_dev * rows - 1) // (list_dev * rows))
    total = rows * list_dev * capacity
    flat = probes.reshape(-1)
    count = flat.shape[0]
    pair_query = jnp.arange(count, dtype=jnp.int32) // nprobe
    rank = earlier_equal(flat)
    cold_id = flat - hot_count
    is_cold = cold_id >= 0
    slot = jnp.where(is_cold, cold_id * capacity + rank, total)
    outgoing = (
        jnp.zeros((total, width), jnp.bfloat16).at[slot].set(queries[pair_query], mode="drop")
    )
    outgoing = outgoing.reshape(rows, list_dev, capacity, width)
    arrived = lax.all_to_all(outgoing, "row", split_axis=0, concat_axis=0, tiled=True)
    scores = jnp.einsum("slcd,lvd->slcv", arrived, cold_lists, preferred_element_type=jnp.float32)
    reading = jnp.minimum(slot, total - 1)
    returned = lax.all_to_all(scores, "row", split_axis=0, concat_axis=0, tiled=True).reshape(
        total, lsize
    )
    cold_rows = returned[reading]
    hot_all = hot_scores(queries, hot_lists)
    hot_pick = jnp.clip(probes, 0, hot_count - 1)
    hot_rows = jnp.take_along_axis(hot_all, hot_pick[:, :, None], axis=1).reshape(count, lsize)
    merged = jnp.where(is_cold[:, None], cold_rows, hot_rows).reshape(qcount, nprobe * lsize)
    return lax.top_k(merged, TOPK)[0]


def solution(mesh):
    placed = (
        P(("tenant", "row"), None),
        P(("tenant", "row"), None),
        P("tenant", None, None),
        P(("tenant", "row"), None, None),
    )
    return jax.shard_map(
        shards, mesh=mesh, in_specs=placed, out_specs=P(("tenant", "row"), None), check_vma=False
    )
```

profile of v0, /device:TPU:538, one launch (start us, length us, event | category | flops | bytes accessed | tf_op | source)
XLA Modules:
  0.0 415.5 jit_solution(14267400865258127704)
XLA Ops:
  2.6 18.6 %while.12 = (s32[]{:T(128)}, s32[4,512]{1,0:T(4,128)S(1)}, s32[4]{0:T(128)S(1)}, s32[2048]{0:T(1024)S(1)}, s32[128,16]{1,0:T(8,128)}, /*index=5*/s32[2048]{0:T(1024)S(1)}, s32[]{:T(128)}, s32[]{:T(128)}, s32[]{:T(128)}) while((s32[]{:T(128)}, s32[4,512]{1,0:T(4,128)S(1)}, s32[4]{0:T(128)S(1)}, s32[2048]{0:T(1024)S(1)}, ...), condition=%wide.wide.region_2.3_spmd.clone, body=%wide.wide.region_0.2_spmd.clone.sunk | while | flops 5242885 | bytes 24727 | solution.py:33
  6.1 1.1 convert_reduce_fusion.3
  10.7 1.1 convert_reduce_fusion.3
  20.0 1.1 convert_reduce_fusion.3
  21.6 26.7 %scatter_custom_fusion = bf16[4096,256]{1,0:T(8,128)(2,1)} fusion(s32[2048]{0:T(1024)S(1)} %bitcast.44, bf16[128,256]{1,0:T(8,128)(2,1)} %param.6, s32[2048]{0:T(1024)S(1)} %broadcast_clamp_fusion.1, bf16[]{:T(256)} %constant.55.clone.1), kind=kCustom, calls=%fused_computation.12 | custom fusion | bytes 2097664 | tf_op jit(solution)/shard_map/scatter | solution.py:51
  48.4 4.0 reshape.157
  52.3 74.2 %all_to_all.10 = bf16[128,8,4,256]{3,2,1,0:T(4,128)(2,1)S(1)} all-to-all(bf16[128,8,4,256]{3,2,1,0:T(4,128)(2,1)} %reshape.157), channel_id=1, replica_groups=mesh['tenant'=2,'row'=128] {'row'}, dimensions={0} | all-to-all | bytes 4194304 | tf_op jit(solution)/shard_map/all_to_all | solution.py:54
  126.6 2.5 convolution_bitcast_fusion
  129.1 4.7 %copy.34 = f32[128,8,4,256]{3,2,1,0:T(4,128)} copy(f32[128,8,4,256]{3,0,2,1:T(8,128)S(1)} %convolution_bitcast_fusion) | data formatting | bytes 8388608 | tf_op jit(solution)/shard_map/slcd,lvd->slcv/transpose | solution.py:55
  133.8 13.2 %all-to-all-start.1 = ((f32[128,8,4,256]{3,2,1,0:T(4,128)}), f32[128,8,4,256]{3,2,1,0:T(4,128)}, u32[]{:S(2)}, u32[]{:S(2)}) async-start(f32[128,8,4,256]{3,2,1,0:T(4,128)} %copy.34), calls=%async_computation.1 | async-start | bytes 8388608 | tf_op jit(solution)/shard_map/all_to_all | solution.py:57
  148.7 2.6 copy.37
  151.5 40.9 %gather_fusion.1 = f32[2048,256]{1,0:T(8,128)} fusion(f32[128,16,256]{2,1,0:T(8,128)} %copy.37, s32[2048]{0:T(1024)S(1)} %reshape.175), kind=kCustom, calls=%fused_computation.2 | custom fusion | bytes 4210688 | tf_op jit(solution)/shard_map/jit(take_along_axis)/gather | solution.py:63
  192.4 1.9 broadcast_select_fusion
  194.4 3.0 copy.45
  197.4 64.9 %all-to-all-done.1 = f32[128,8,4,256]{3,2,1,0:T(4,128)} async-done(((f32[128,8,4,256]{3,2,1,0:T(4,128)}), f32[128,8,4,256]{3,2,1,0:T(4,128)}, u32[]{:S(2)}, u32[]{:S(2)}) %all-to-all-start.1) | async-done | bytes 4194336 | tf_op jit(solution)/shard_map/all_to_all | solution.py:57
  262.3 5.3 %reshape.158 = f32[4096,256]{1,0:T(8,128)} reshape(f32[128,8,4,256]{3,2,1,0:T(4,128)} %all-to-all-done.1) | data formatting | bytes 8388608 | tf_op jit(solution)/shard_map/reshape | solution.py:57
  267.6 10.7 %gather_fusion = f32[2048,256]{1,0:T(8,128)} fusion(f32[4096,256]{1,0:T(8,128)} %reshape.158, s32[2048]{0:T(1024)S(1)} %broadcast_clamp_fusion), kind=kCustom, calls=%fused_computation.1 | custom fusion | bytes 4202496 | tf_op jit(solution)/shard_map/gather | solution.py:60
  278.3 2.7 gather.14
  281.1 3.9 select_n.90
  284.9 2.9 copy.39
  287.9 1.4 iota.21.clone
  289.3 121.8 %top_k.9 = (f32[128,4096]{0,1:T(8,128)}, s32[128,4096]{0,1:T(8,128)}) sort(f32[128,4096]{0,1:T(8,128)} %copy.39, s32[128,4096]{0,1:T(8,128)} %iota.21.clone), dimensions={1}, to_apply=%region_4.5 | sort | flops 9961472 | bytes 8388608 | tf_op jit(solution)/shard_map/top_k | solution.py:65
  411.1 2.9 copy.41
  414.0 1.5 top_k.11
  (50 shorter events, 11.9 us)
Async XLA Ops:
  0.0 147.9 %copy-start = (bf16[16,256,256]{2,1,0:T(8,128)(2,1)S(1)}, bf16[16,256,256]{2,1,0:T(8,128)(2,1)}, u32[]{:S(2)}) copy-start(bf16[16,256,256]{2,1,0:T(8,128)(2,1)} %param.8) | copy-start | bytes 6291460
  0.9 1.6 copy-start.2
  52.3 74.3 %copy-start.1 = (bf16[8,256,256]{2,1,0:T(8,128)(2,1)S(1)}, bf16[8,256,256]{2,1,0:T(8,128)(2,1)}, u32[]{:S(2)}) copy-start(bf16[8,256,256]{2,1,0:T(8,128)(2,1)} %param.9) | copy-start | bytes 3145732
  133.8 14.1 %copy-start.4 = (bf16[128,256]{1,0:T(8,128)(2,1)S(1)}, bf16[128,256]{1,0:T(8,128)(2,1)}, u32[]{:S(2)}) copy-start(bf16[128,256]{1,0:T(8,128)(2,1)} %param.6) | copy-start | bytes 196612
  133.8 128.6 %all-to-all-start.1 = ((f32[128,8,4,256]{3,2,1,0:T(4,128)}), f32[128,8,4,256]{3,2,1,0:T(4,128)}, u32[]{:S(2)}, u32[]{:S(2)}) async-start(f32[128,8,4,256]{3,2,1,0:T(4,128)} %copy.34), calls=%async_computation.1 | async-start | bytes 8388608 | tf_op jit(solution)/shard_map/all_to_all | solution.py:57
  148.7 2.6 copy-start.3
where the time goes:
time: 418 us; the launch traced here: 415 us
  other arithmetic  136 us (33%)
  local copies, waits for them, and re-layouts  115 us (28%)
  blocking collectives  74.2 us (18%)
  waiting for transfers between devices  64.9 us (16%)
  starting transfers between devices  13.2 us (3%)
  loops' own time  8.4 us (2%)
    top_k x1, other arithmetic, shards(): return lax.top_k(merged, TOPK)[0]  122 us
    all_to_all x1, blocking collectives, shards(): lax.all_to_all(outgoing, 'row', split_axis=0, concat_axis=0, tiled=True)  74.2 us
    all_to_all x1, waiting for transfers between devices, shards(): lax.all_to_all(scores, 'row', split_axis=0, concat_axis=0, tiled=True)  64.9 us
    gather x3, local copies, waits for them, and re-layouts, shards(): jnp.take_along_axis(hot_all, hot_pick[:, :, None], axis=1)  41.1 us
    scatter x1, local copies, waits for them, and re-layouts, shards(): jnp.zeros((total, width), jnp.bfloat16).at[slot]  26.7 us
    gather x2, local copies, waits for them, and re-layouts, shards(): cold_rows = returned[reading]  13.5 us
    all_to_all x1, starting transfers between devices, shards(): lax.all_to_all(scores, 'row', split_axis=0, concat_axis=0, tiled=True)  13.2 us
    another operation x1, loops' own time, earlier_equal(): return lax.map(one_block, starts).reshape(count)  8.4 us
  transfers between devices with their start and end apart: 1, of which 1 were waited for; matrix products, arithmetic and copies ran while one was open for 12% of the time, Pallas kernels for 0%

commit v1 on v0

v1 whole, which is shorter than its diff:
```python
import functools
import math

import jax
import jax.numpy as jnp
from jax import lax
from jax.experimental import pallas as pl
from jax.experimental.pallas import tpu as pltpu
from jax.sharding import PartitionSpec as P

MESH = pl.DeviceIdType.MESH
TOPK = 128
LANES = 128
SUB = 8
NEG = float("-inf")


def odd_even(n):
    pairs = []

    def merge(lo, hi, step):
        jump = step * 2
        if jump < hi - lo:
            merge(lo, hi, jump)
            merge(lo + step, hi, jump)
            pairs.extend((i, i + step) for i in range(lo + step, hi - step, jump))
        else:
            pairs.append((lo, lo + step))

    def sort(lo, hi):
        if hi - lo >= 1:
            mid = lo + (hi - lo) // 2
            sort(lo, mid)
            sort(mid + 1, hi)
            merge(lo, hi, 1)

    sort(0, n - 1)
    return pairs


def bitonic(values, distances):
    values = list(values)
    for d in distances:
        for i in range(len(values)):
            if i & d == 0:
                a, b = values[i], values[i + d]
                values[i], values[i + d] = jnp.maximum(a, b), jnp.minimum(a, b)
    return values


def row(base, i):
    return pl.ds(pl.multiple_of((base + i) * SUB, SUB), SUB)


def sort_groups(ref, groups, n=32):
    pairs = odd_even(n)

    def body(g, _):
        v = [ref[row(g * n, i), :] for i in range(n)]
        for a, b in pairs:
            v[a], v[b] = jnp.maximum(v[a], v[b]), jnp.minimum(v[a], v[b])
        for i in range(n):
            ref[row(g * n, i), :] = v[i]
        return 0

    lax.fori_loop(0, groups, body, 0)


def merge_full_32(src, dst, count):
    def body(g, _):
        base = g * 64
        for pick, at in ((jnp.maximum, 0), (jnp.minimum, 32)):
            v = [pick(src[row(base, i), :], src[row(base + 32, 31 - i), :]) for i in range(32)]
            v = bitonic(v, (16, 8, 4, 2, 1))
            for i in range(32):
                dst[row(base + at, i), :] = v[i]
        return 0

    lax.fori_loop(0, count, body, 0)


def half_64(src, a, b, outer, inner):
    v = []
    for i in range(32):
        low = outer(src[row(a, i), :], src[row(b, 63 - i), :])
        high = outer(src[row(a, i + 32), :], src[row(b, 31 - i), :])
        v.append(inner(low, high))
    return bitonic(v, (16, 8, 4, 2, 1))


def merge_full_64(src, dst, count):
    def body(g, _):
        base = g * 128
        at = 0
        for outer in (jnp.maximum, jnp.minimum):
            for inner in (jnp.maximum, jnp.minimum):
                v = half_64(src, base, base + 64, outer, inner)
                for i in range(32):
                    dst[row(base + at, i), :] = v[i]
                at += 32
        return 0

    lax.fori_loop(0, count, body, 0)


def merge_top_128(a, a0, b, b0, dst, d0, mid, shift=0):
    def first(g, _):
        v = []
        for k in range(8):
            other = b[row(b0 + 127 - g - 16 * k, 0), :]
            if shift:
                other = pltpu.roll(other, shift, 0)
            v.append(jnp.maximum(a[row(a0 + g + 16 * k, 0), :], other))
        v = bitonic(v, (4, 2, 1))
        for k in range(8):
            mid[row(g + 16 * k, 0), :] = v[k]
        return 0

    lax.fori_loop(0, 16, first, 0, unroll=2)

    def second(g, _):
        v = bitonic([mid[row(g * 16, i), :] for i in range(16)], (8, 4, 2, 1))
        for i in range(16):
            dst[row(d0 + g * 16, i), :] = v[i]
        return 0

    lax.fori_loop(0, 8, second, 0, unroll=2)


def sort_top_128(x, y, mid):
    sort_groups(x, 8)
    merge_full_32(x, y, 4)
    merge_full_64(y, x, 2)
    merge_top_128(x, 0, x, 128, y, 0, mid)


def prepare(rows, list_dev, hot, cap, probes_ref, queries_ref, block_ref, enc_ref, table):
    qcount, nprobe = probes_ref.shape
    cold = rows * list_dev
    lane = lax.broadcasted_iota(jnp.int32, (qcount, cold), 1)
    ids = (lane % rows) * list_dev + lane // rows + hot
    probes = probes_ref[...]
    named = jnp.zeros((qcount, cold), jnp.float32)
    for j in range(nprobe):
        named = jnp.where(probes[:, j : j + 1] == ids, 1.0, named)
    below = lax.broadcasted_iota(jnp.int32, (qcount, qcount), 1) < lax.broadcasted_iota(
        jnp.int32, (qcount, qcount), 0
    )
    rank = jnp.dot(
        below.astype(jnp.float32).astype(jnp.bfloat16),
        named.astype(jnp.bfloat16),
        preferred_element_type=jnp.float32,
    )
    number = lax.broadcasted_iota(jnp.int32, (qcount, cold), 0).astype(jnp.float32) + 1.0
    for r in range(cap):
        held = jnp.where((named > 0) & (rank == float(r)), number, 0.0)
        line = jnp.sum(held, axis=0, keepdims=True)
        for l in range(list_dev):
            e = l * cap + r
            table[e : e + 1, :] = line[:, l * rows : (l + 1) * rows]
    half = list_dev * cap // 2
    block_ref[0:qcount, :] = queries_ref[...]
    block_ref[qcount : qcount + half, 0:rows] = table[0:half, :].astype(jnp.bfloat16)
    block_ref[qcount : qcount + half, rows : 2 * rows] = table[half : 2 * half, :].astype(
        jnp.bfloat16
    )
    columns = lax.broadcasted_iota(jnp.int32, (qcount, LANES), 1)
    enc = jnp.zeros((qcount, LANES), jnp.float32)
    for j in range(nprobe):
        p = probes[:, j : j + 1]
        mine = jnp.sum(jnp.where(p == ids, rank, 0.0), axis=1, keepdims=True)
        pf = p.astype(jnp.float32)
        code = jnp.where(p < hot, -1.0 - pf, (pf - hot) * cap + mine)
        enc = jnp.where(columns == j, code, enc)
    enc_ref[...] = jnp.transpose(enc)[0:nprobe, :].astype(jnp.int32)


def exchange(rows, side, list_dev, cap, block_ref, lists_ref, out_ref, got, picked, x, y, mid, back,
             send_sem, own_sem, sib_sem, back_sem, ret_sem):
    me = lax.axis_index("row")
    mx, my, c = me // (2 * side), (me // 2) % side, me % 2
    chips = side * side
    depth = block_ref.shape[0]
    half = list_dev * cap // 2
    qcount = depth - half
    slots = list_dev * cap
    pairs = list_dev // 2

    def at(dx, dy, core):
        return (((mx + dx) % side) * side + (my + dy) % side) * 2 + core

    barrier = pltpu.get_barrier_semaphore()

    def greet(k, _):
        pl.semaphore_signal(barrier, 1, device_id={"row": (me + k) % rows}, device_id_type=MESH)
        return 0

    lax.fori_loop(1, rows, greet, 0)
    pl.semaphore_wait(barrier, rows - 1)

    def along(da, db):
        return at(da * (1 - c) + db * c, da * c + db * (1 - c), c)

    def push(src, da, db, to_a, to_b):
        slot = ((da - to_a) % side) * side + (db - to_b) % side
        pltpu.make_async_remote_copy(
            src, got.at[c, slot], send_sem, own_sem.at[slot],
            device_id={"row": along(to_a % side, to_b % side)}, device_id_type=MESH,
        ).start()

    def signed(d):
        return d if d <= side // 2 else d - side

    def forward(src, da, db):
        sa, sb = signed(da), signed(db)
        far = side // 2
        if db == 0:
            if sa <= 0 and -sa + 1 <= far and da != far:
                push(src, da, db, 1, 0)
            if sa >= 0 and sa + 1 <= far - 1:
                push(src, da, db, -1, 0)
        plus, minus = (far, far - 1) if da % 2 == 0 else (far - 1, far)
        came_plus = db == 0 or sb < 0
        came_minus = db == 0 or (sb > 0 and db != far)
        if came_plus and (0 if db == 0 else -sb) + 1 <= plus:
            push(src, da, db, 0, 1)
        if came_minus and (0 if db == 0 else sb) + 1 <= minus:
            push(src, da, db, 0, -1)

    def to_sibling(src, slot):
        pltpu.make_async_remote_copy(
            src, got.at[c, slot], send_sem, sib_sem.at[slot],
            device_id={"row": at(0, 0, 1 - c)}, device_id_type=MESH,
        ).start()

    forward(block_ref, 0, 0)
    to_sibling(block_ref, 0)
    got[c, 0] = block_ref[...]
    order = [(a, b) for a in range(side) for b in range(side) if (a, b) != (0, 0)]
    order.sort(key=lambda o: (abs(signed(o[0])) + abs(signed(o[1])), abs(signed(o[1])), o))
    for da, db in order:
        slot = da * side + db
        here = got.at[c, slot]
        pltpu.make_async_remote_copy(
            here, here, send_sem, own_sem.at[slot], device_id={"row": me}, device_id_type=MESH
        ).wait_recv()
        forward(here, da, db)
        to_sibling(here, slot)

    share = chips // (LANES // SUB)
    per = chips // share
    choose = (lax.broadcasted_iota(jnp.int32, (rows, LANES), 0) == me).astype(jnp.float32).astype(jnp.bfloat16)
    number = lax.broadcasted_iota(jnp.int32, (slots, qcount), 1).astype(jnp.float32) + 1.0
    odd = (lax.broadcasted_iota(jnp.int32, (lists_ref.shape[1], 2 * LANES), 1) // cap) % 2 == 1

    def batch(b, _):
        def take(k, _):
            i = b * per + k
            for t in range(2):
                slot = i if t == 0 else (i % side) * side + i // side
                here = got.at[t, slot]

                @pl.when((c != t))
                def _():
                    pltpu.make_async_remote_copy(
                        here, here, send_sem, sib_sem.at[slot], device_id={"row": me}, device_id_type=MESH
                    ).wait_recv()

                table = jnp.concatenate(
                    [got[t, slot, qcount:depth, 0:rows], got[t, slot, qcount:depth, rows : 2 * rows]], axis=0
                )
                wide = jnp.dot(table, choose, preferred_element_type=jnp.float32)
                hits = (wide == number).astype(jnp.float32).astype(jnp.bfloat16)
                chosen = jnp.dot(hits, got[t, slot, 0:qcount, :], preferred_element_type=jnp.float32)
                for m in range(pairs):
                    picked[m, pl.ds(pl.multiple_of(t * LANES + k * SUB, SUB), SUB), :] = chosen[
                        m * SUB : (m + 1) * SUB, :
                    ]
            return 0

        lax.fori_loop(0, per, take, 0)

        for m in range(pairs):
            right = picked[m].astype(jnp.bfloat16)
            dims = (((1,), (1,)), ((), ()))
            even_s = lax.dot_general(lists_ref[2 * m], right, dims, preferred_element_type=jnp.float32)
            odd_s = lax.dot_general(lists_ref[2 * m + 1], right, dims, preferred_element_type=jnp.float32)
            s = jnp.where(odd, odd_s, even_s)
            for t in range(2):
                x[pl.ds(2 * m + t, s.shape[0], stride=SUB), :] = s[:, t * LANES : (t + 1) * LANES]
        sort_top_128(x, y, mid)
        for m in range(pairs):
            for t in range(2):
                sorted_rows = jnp.transpose(y[pl.ds(2 * m + t, TOPK, stride=SUB), :])
                back[pl.ds(b * per, per), t, m * SUB : (m + 1) * SUB, :] = sorted_rows.reshape(per, SUB, TOPK)

        def give(k, _):
            i = b * per + k
            for t in range(2):

                @pl.when((i != 0) | (c != t))
                def _():
                    pltpu.make_async_remote_copy(
                        back.at[i, t], out_ref.at[me], back_sem, ret_sem,
                        device_id={"row": at(i // side, i % side, t)}, device_id_type=MESH,
                    ).start()
            return 0

        lax.fori_loop(0, per, give, 0)
        return 0

    lax.fori_loop(0, share, batch, 0)
    out_ref[me] = back[0, c]

    def drain(k, _):
        here = got.at[c, 0]
        pltpu.make_async_remote_copy(
            here, here, send_sem, own_sem.at[0], device_id={"row": me}, device_id_type=MESH
        ).wait_send()
        return 0

    lax.fori_loop(0, 2 * chips - 1, drain, 0)
    whole = out_ref.at[pl.ds(0, rows - 1)]
    done = pltpu.make_async_remote_copy(
        whole, whole, back_sem, ret_sem, device_id={"row": me}, device_id_type=MESH
    )
    done.wait_send()
    done.wait_recv()


def finish(enc_smem, enc_ref, rows_ref, queries_ref, hot_ref, out_ref, buf, x, y, mid, lists_a, lists_b):
    nprobe, qcount = enc_ref.shape
    hot = hot_ref.shape[0]
    enc = enc_ref[...]

    def gather(j, _):
        def one(q, _):
            at = jnp.maximum(enc_smem[j, q], 0)
            buf[pl.ds(j * qcount + q, 1), :] = rows_ref[pl.ds(at, 1), :]
            return 0

        lax.fori_loop(0, qcount, one, 0, unroll=16)
        return 0

    lax.fori_loop(0, nprobe, gather, 0)
    for j in range(nprobe):
        dst = lists_a if j < SUB else lists_b
        flat = jnp.transpose(buf[j * qcount : (j + 1) * qcount, :])
        flat = jnp.where(enc[j : j + 1, :] < 0, NEG, flat)
        dst[pl.ds(j % SUB, TOPK, stride=SUB), :] = flat
    merge_top_128(lists_a, 0, lists_b, 0, lists_a, 0, mid)
    for g in range(hot // SUB):
        for s in range(SUB):
            h = g * SUB + s
            scores = lax.dot_general(
                hot_ref[h], queries_ref[...], (((1,), (1,)), ((), ())), preferred_element_type=jnp.float32
            )
            asked = jnp.max((enc == -1 - h).astype(jnp.float32), axis=0, keepdims=True)
            x[pl.ds(s, scores.shape[0], stride=SUB), :] = jnp.where(asked > 0, scores, NEG)
        sort_top_128(x, y, mid)
        merge_top_128(lists_a, 0, y, 0, lists_a, 0, mid)
    for shift in (4, 2, 1):
        merge_top_128(lists_a, 0, lists_a, 0, lists_b, 0, mid, shift)
        lists_a, lists_b = lists_b, lists_a
    out_ref[...] = jnp.transpose(lists_a[pl.ds(0, TOPK, stride=SUB), :])


def shards(queries, probes, hot_lists, cold_lists):
    rows = lax.axis_size("row")
    side = math.isqrt(rows // 2)
    qcount, nprobe = probes.shape
    width = queries.shape[1]
    list_dev, lsize = cold_lists.shape[0], cold_lists.shape[1]
    hot = hot_lists.shape[0]
    cap = 2 * ((qcount * nprobe + list_dev * rows - 1) // (list_dev * rows))
    slots = list_dev * cap
    depth = qcount + slots // 2
    vmem = pl.BlockSpec(memory_space=pltpu.VMEM)
    limit = 60 * 2**20
    f32 = jnp.float32
    column = pltpu.VMEM((lsize * SUB, LANES), f32)
    small = pltpu.VMEM((TOPK * SUB, LANES), f32)

    block, enc = pl.pallas_call(
        functools.partial(prepare, rows, list_dev, hot, cap),
        out_shape=(
            jax.ShapeDtypeStruct((depth, width), jnp.bfloat16),
            jax.ShapeDtypeStruct((nprobe, qcount), jnp.int32),
        ),
        in_specs=[vmem] * 2,
        out_specs=(vmem, vmem),
        scratch_shapes=[pltpu.VMEM((slots, rows), f32)],
        compiler_params=pltpu.CompilerParams(vmem_limit_bytes=limit),
    )(probes, queries)

    returned = pl.pallas_call(
        functools.partial(exchange, rows, side, list_dev, cap),
        out_shape=jax.ShapeDtypeStruct((rows, slots, TOPK), f32),
        in_specs=[vmem] * 2,
        out_specs=vmem,
        scratch_shapes=[
            pltpu.VMEM((2, side * side, depth, width), jnp.bfloat16),
            pltpu.VMEM((list_dev // 2, 2 * LANES, width), f32),
            column,
            column,
            small,
            pltpu.VMEM((side * side, 2, slots, TOPK), f32),
            pltpu.SemaphoreType.DMA,
            pltpu.SemaphoreType.DMA((side * side,)),
            pltpu.SemaphoreType.DMA((side * side,)),
            pltpu.SemaphoreType.DMA,
            pltpu.SemaphoreType.DMA,
        ],
        compiler_params=pltpu.CompilerParams(collective_id=0, has_side_effects=True, vmem_limit_bytes=limit),
    )(block, cold_lists)

    return pl.pallas_call(
        finish,
        out_shape=jax.ShapeDtypeStruct((qcount, TOPK), f32),
        in_specs=[pl.BlockSpec(memory_space=pltpu.SMEM)] + [vmem] * 4,
        out_specs=vmem,
        scratch_shapes=[pltpu.VMEM((nprobe * qcount, TOPK), f32), column, column, small, small, small],
        compiler_params=pltpu.CompilerParams(vmem_limit_bytes=limit),
    )(enc, enc, returned.reshape(rows * slots, TOPK), queries, hot_lists)


def solution(mesh):
    placed = (
        P(("tenant", "row"), None),
        P(("tenant", "row"), None),
        P("tenant", None, None),
        P(("tenant", "row"), None, None),
    )
    return jax.shard_map(
        shards, mesh=mesh, in_specs=placed, out_specs=P(("tenant", "row"), None), check_vma=False
    )
```

time: 418 us -> 167 us (0.40)
  the two profiles are of different devices: /device:TPU:538 before, /device:TPU:513 now
where the time goes in v1:
time: 167 us
  Pallas kernels  165 us (99%)
    pallas_call x1, Pallas kernels, shards(): pl.pallas_call(functools.partial(exchange, rows, side, list_dev, cap), ou...  145 us
    pallas_call x1, Pallas kernels, shards(): pl.pallas_call(finish, out_shape=jax.ShapeDtypeStruct((qcount, TOPK), f32...  14.7 us
    pallas_call x1, Pallas kernels, shards(): pl.pallas_call(functools.partial(prepare, rows, list_dev, hot, cap), out_...  5.62 us

profile of v1, /device:TPU:513, one launch (start us, length us, event | category | flops | bytes accessed | tf_op | source)
XLA Modules:
  0.0 166.7 jit_solution(15516895617310091699)
XLA Ops:
  0.0 1.4 copy.5.probes_ref
  1.4 5.6 %shard_map.46 = (bf16[144,256]{1,0:T(8,128)(2,1)}, s32[16,128]{1,0:T(8,128)}) custom-call(s32[128,16]{1,0:T(8,128)} %copy.5.probes_ref, bf16[128,256]{1,0:T(8,128)(2,1)} %queries_ref.3), custom_call_target="tpu_custom_call" | custom-call | tf_op jit(solution)/shard_map/pallas_call | solution.py:384
  7.0 144.9 %shard_map.47 = f32[128,32,128]{2,1,0:T(8,128)} custom-call(bf16[144,256]{1,0:T(8,128)(2,1)} %get-tuple-element.8.block_ref, bf16[8,256,256]{2,1,0:T(8,128)(2,1)} %lists_ref.1), custom_call_target="tpu_custom_call" | custom-call | tf_op jit(solution)/shard_map/pallas_call | solution.py:396
  152.0 14.7 %shard_map.48 = f32[128,128]{1,0:T(8,128)} custom-call(s32[16,128]{1,0:T(8,128)} %get-tuple-element.7.enc_smem.enc_ref, s32[16,128]{1,0:T(8,128)} %get-tuple-element.7.enc_smem.enc_ref, f32[4096,128]{1,0:T(8,128)} %bitcast.1, bf16[128,256]{1,0:T(8,128)(2,1)} %queries_ref.3, bf16[16,256,256]{2,1,0:T(8,128)(2,1)} %hot_ref.1), custom_call_target="tpu_custom_call" | custom-call | tf_op jit(solution)/shard_map/pallas_call | solution.py:417

commit v2 on v1

v2 whole, which is shorter than its diff:
```python
import functools
import math

import jax
import jax.numpy as jnp
from jax import lax
from jax.experimental import pallas as pl
from jax.experimental.pallas import tpu as pltpu
from jax.sharding import PartitionSpec as P

MESH = pl.DeviceIdType.MESH
TOPK = 128
LANES = 128
SUB = 8
NEG = float("-inf")


def odd_even(n):
    pairs = []

    def merge(lo, hi, step):
        jump = step * 2
        if jump < hi - lo:
            merge(lo, hi, jump)
            merge(lo + step, hi, jump)
            pairs.extend((i, i + step) for i in range(lo + step, hi - step, jump))
        else:
            pairs.append((lo, lo + step))

    def sort(lo, hi):
        if hi - lo >= 1:
            mid = lo + (hi - lo) // 2
            sort(lo, mid)
            sort(mid + 1, hi)
            merge(lo, hi, 1)

    sort(0, n - 1)
    return pairs


def bitonic(values, distances):
    values = list(values)
    for d in distances:
        for i in range(len(values)):
            if i & d == 0:
                a, b = values[i], values[i + d]
                values[i], values[i + d] = jnp.maximum(a, b), jnp.minimum(a, b)
    return values


def row(base, i):
    return pl.ds(pl.multiple_of((base + i) * SUB, SUB), SUB)


def sort_groups(ref, start, stop, n=32):
    pairs = odd_even(n)

    def body(g, _):
        v = [ref[row(g * n, i), :] for i in range(n)]
        for a, b in pairs:
            v[a], v[b] = jnp.maximum(v[a], v[b]), jnp.minimum(v[a], v[b])
        for i in range(n):
            ref[row(g * n, i), :] = v[i]
        return 0

    lax.fori_loop(start, stop, body, 0)


def merge_full_32(src, dst, count):
    def body(g, _):
        base = g * 64
        for pick, at in ((jnp.maximum, 0), (jnp.minimum, 32)):
            v = [pick(src[row(base, i), :], src[row(base + 32, 31 - i), :]) for i in range(32)]
            v = bitonic(v, (16, 8, 4, 2, 1))
            for i in range(32):
                dst[row(base + at, i), :] = v[i]
        return 0

    lax.fori_loop(0, count, body, 0)


def half_64(src, a, b, outer, inner):
    v = []
    for i in range(32):
        low = outer(src[row(a, i), :], src[row(b, 63 - i), :])
        high = outer(src[row(a, i + 32), :], src[row(b, 31 - i), :])
        v.append(inner(low, high))
    return bitonic(v, (16, 8, 4, 2, 1))


def merge_full_64(src, dst, count):
    def body(g, _):
        base = g * 128
        at = 0
        for outer in (jnp.maximum, jnp.minimum):
            for inner in (jnp.maximum, jnp.minimum):
                v = half_64(src, base, base + 64, outer, inner)
                for i in range(32):
                    dst[row(base + at, i), :] = v[i]
                at += 32
        return 0

    lax.fori_loop(0, count, body, 0)


def merge_top_128(a, a0, b, b0, dst, d0, mid, shift=0):
    def first(g, _):
        v = []
        for k in range(8):
            other = b[row(b0 + 127 - g - 16 * k, 0), :]
            if shift:
                other = pltpu.roll(other, shift, 0)
            v.append(jnp.maximum(a[row(a0 + g + 16 * k, 0), :], other))
        v = bitonic(v, (4, 2, 1))
        for k in range(8):
            mid[row(g + 16 * k, 0), :] = v[k]
        return 0

    lax.fori_loop(0, 16, first, 0, unroll=2)

    def second(g, _):
        v = bitonic([mid[row(g * 16, i), :] for i in range(16)], (8, 4, 2, 1))
        for i in range(16):
            dst[row(d0 + g * 16, i), :] = v[i]
        return 0

    lax.fori_loop(0, 8, second, 0, unroll=2)


def sort_top_128(x, y, mid):
    sort_groups(x, 0, 4)
    yield
    sort_groups(x, 4, 8)
    yield
    merge_full_32(x, y, 4)
    yield
    merge_full_64(y, x, 2)
    yield
    merge_top_128(x, 0, x, 128, y, 0, mid)
    yield


def exchange(rows, side, cap, probes_ref, queries_ref, lists_ref, hot_ref, out_ref, enc_ref, hot_out, block, table, ranks,
             got, picked, x, y, mid, back, send_sem, own_sem, sib_sem, back_sem, ret_sem):
    me = lax.axis_index("row")
    mx, my, c = me // (2 * side), (me // 2) % side, me % 2
    chips = side * side
    list_dev, lsize = lists_ref.shape[0], lists_ref.shape[1]
    hot = hot_ref.shape[0]
    nprobe, qcount = probes_ref.shape
    slots = list_dev * cap
    half = slots // 2
    depth = qcount + half
    pairs = list_dev // 2
    cold = rows * list_dev
    f32, bf16 = jnp.float32, jnp.bfloat16
    last = (((1,), (1,)), ((), ()))

    def at(dx, dy, core):
        return (((mx + dx) % side) * side + (my + dy) % side) * 2 + core

    barrier = pltpu.get_barrier_semaphore()

    def greet(k, _):
        pl.semaphore_signal(barrier, 1, device_id={"row": (me + k) % rows}, device_id_type=MESH)
        return 0

    lax.fori_loop(1, rows, greet, 0)

    wide_probes = jnp.concatenate(
        [probes_ref[...].astype(f32), jnp.zeros((LANES - nprobe, qcount), f32)], axis=0
    )
    probes = jnp.transpose(wide_probes)
    lane = lax.broadcasted_iota(jnp.int32, (qcount, cold), 1)
    ids = ((lane % rows) * list_dev + lane // rows + hot).astype(f32)
    named = jnp.zeros((qcount, cold), f32)
    for j in range(nprobe):
        named = jnp.where(probes[:, j : j + 1] == ids, 1.0, named)
    below = lax.broadcasted_iota(jnp.int32, (qcount, qcount), 1) < lax.broadcasted_iota(
        jnp.int32, (qcount, qcount), 0
    )
    rank = jnp.dot(below.astype(f32).astype(bf16), named.astype(bf16), preferred_element_type=f32)
    ranks[...] = rank
    order_of = lax.broadcasted_iota(jnp.int32, (qcount, cold), 0).astype(f32) + 1.0
    for r in range(cap):
        held = jnp.where((named > 0) & (rank == float(r)), order_of, 0.0)
        line = jnp.sum(held, axis=0, keepdims=True)
        for l in range(list_dev):
            e = l * cap + r
            table[e : e + 1, :] = line[:, l * rows : (l + 1) * rows]
    block[qcount:depth, 0:rows] = table[0:half, :].astype(bf16)
    block[qcount:depth, rows : 2 * rows] = table[half : 2 * half, :].astype(bf16)
    block[0:qcount, :] = queries_ref[...]
    got[c, 0] = block[...]

    pl.semaphore_wait(barrier, rows - 1)

    def along(da, db):
        return at(da * (1 - c) + db * c, da * c + db * (1 - c), c)

    def push(src, da, db, to_a, to_b):
        slot = ((da - to_a) % side) * side + (db - to_b) % side
        pltpu.make_async_remote_copy(
            src, got.at[c, slot], send_sem, own_sem.at[slot],
            device_id={"row": along(to_a % side, to_b % side)}, device_id_type=MESH,
        ).start()

    def signed(d):
        return d if d <= side // 2 else d - side

    def forward(src, da, db):
        sa, sb = signed(da), signed(db)
        far = side // 2
        if db == 0:
            if sa <= 0 and -sa + 1 <= far:
                push(src, da, db, 1, 0)
            if sa >= 0 and sa + 1 <= far - 1:
                push(src, da, db, -1, 0)
        plus, minus = (far, far - 1) if da % 2 == 0 else (far - 1, far)
        came_plus = db == 0 or sb < 0
        came_minus = db == 0 or (sb > 0 and db != far)
        if came_plus and (0 if db == 0 else -sb) + 1 <= plus:
            push(src, da, db, 0, 1)
        if came_minus and (0 if db == 0 else sb) + 1 <= minus:
            push(src, da, db, 0, -1)

    def to_sibling(src, slot):
        pltpu.make_async_remote_copy(
            src, got.at[c, slot], send_sem, sib_sem.at[slot],
            device_id={"row": at(0, 0, 1 - c)}, device_id_type=MESH,
        ).start()

    def await_block(t, slot, sem):
        here = got.at[t, slot]
        pltpu.make_async_remote_copy(
            here, here, send_sem, sem.at[slot], device_id={"row": me}, device_id_type=MESH
        ).wait_recv()

    order = [(a, b) for a in range(side) for b in range(side)]
    order.sort(key=lambda o: (abs(signed(o[0])) + abs(signed(o[1])), abs(signed(o[1])), o))
    per = LANES // SUB
    step = 4

    choose = (lax.broadcasted_iota(jnp.int32, (rows, LANES), 0) == me).astype(f32).astype(bf16)
    number = lax.broadcasted_iota(jnp.int32, (slots, qcount), 1).astype(f32) + 1.0
    odd = (lax.broadcasted_iota(jnp.int32, (lsize, 2 * LANES), 1) // cap) % 2 == 1

    def slot_of(t, chip):
        return chip[t] * side + chip[1 - t]

    def positions():
        columns = lax.broadcasted_iota(jnp.int32, (qcount, LANES), 1)
        enc = jnp.zeros((qcount, LANES), f32)
        for j in range(nprobe):
            p = probes[:, j : j + 1]
            mine = jnp.sum(jnp.where(p == ids, ranks[...], 0.0), axis=1, keepdims=True)
            code = jnp.where(p < hot, -1.0 - p, (p - hot) * cap + mine)
            enc = jnp.where(columns == j, code, enc)
        enc_ref[...] = jnp.transpose(enc)[0:nprobe, :].astype(jnp.int32)
        yield

    def hot_work():
        for g in range(hot // SUB):
            for s in range(SUB):
                h = g * SUB + s
                scores = lax.dot_general(hot_ref[h], queries_ref[...], last, preferred_element_type=f32)
                asked = jnp.max((probes_ref[...] == h).astype(f32), axis=0, keepdims=True)
                x[pl.ds(s, lsize, stride=SUB), :] = jnp.where(asked > 0, scores, NEG)
                if s % 4 == 3:
                    yield
            yield from sort_top_128(x, y, mid)
            if g == 0:
                hot_out[...] = y[0 : TOPK * SUB, :]
            else:
                merge_top_128(hot_out, 0, y, 0, hot_out, 0, mid)
            yield

    def batch(b):
        mine = order[b * per : (b + 1) * per]
        for k0 in range(0, per, step):
            some = [(k, t) for k in range(k0, k0 + step) for t in range(2)]
            for t in range(2):

                @pl.when(c != t)
                def _():
                    for k in range(k0, k0 + step):
                        await_block(t, slot_of(t, mine[k]), sib_sem)

            tables = []
            for k, t in some:
                slot = slot_of(t, mine[k])
                tables += [got[t, slot, qcount:depth, 0:rows], got[t, slot, qcount:depth, rows : 2 * rows]]
            wide = jnp.dot(jnp.concatenate(tables, axis=0), choose, preferred_element_type=f32)
            for n, (k, t) in enumerate(some):
                hits = (wide[n * slots : (n + 1) * slots, :] == number).astype(f32).astype(bf16)
                chosen = jnp.dot(hits, got[t, slot_of(t, mine[k]), 0:qcount, :], preferred_element_type=f32)
                for m in range(pairs):
                    low = t * LANES + k * SUB
                    picked[m, low : low + SUB, :] = chosen[m * SUB : (m + 1) * SUB, :]
            yield
        for m in range(pairs):
            right = picked[m].astype(bf16)
            even_s = lax.dot_general(lists_ref[2 * m], right, last, preferred_element_type=f32)
            odd_s = lax.dot_general(lists_ref[2 * m + 1], right, last, preferred_element_type=f32)
            s = jnp.where(odd, odd_s, even_s)
            for t in range(2):
                x[pl.ds(2 * m + t, lsize, stride=SUB), :] = s[:, t * LANES : (t + 1) * LANES]
            yield
        yield from sort_top_128(x, y, mid)
        for m in range(pairs):
            for t in range(2):
                sorted_rows = jnp.transpose(y[pl.ds(2 * m + t, TOPK, stride=SUB), :])
                back[b * per : (b + 1) * per, t, m * SUB : (m + 1) * SUB, :] = sorted_rows.reshape(per, SUB, TOPK)
        yield
        for k in range(per):
            dx, dy = mine[k]
            for t in range(2):

                def give():
                    pltpu.make_async_remote_copy(
                        back.at[b * per + k, t], out_ref.at[me], back_sem, ret_sem,
                        device_id={"row": at(dx, dy, t)}, device_id_type=MESH,
                    ).start()

                if (dx, dy) == (0, 0):
                    pl.when(c != t)(give)
                else:
                    give()
            if k % step == step - 1:
                yield

    forward(block, 0, 0)
    to_sibling(block, 0)

    todo = [positions(), hot_work()]
    batches = [(set(order[b * per : (b + 1) * per]), batch(b)) for b in range(chips // per)]
    passed = {(0, 0)}

    def advance(count):
        while count and (todo or batches):
            if not todo:
                need, work = batches[0]
                if not all((a, b) in passed and (b, a) in passed for a, b in need):
                    return
                batches.pop(0)
                todo.append(work)
            try:
                next(todo[0])
                count -= 1
            except StopIteration:
                todo.pop(0)

    for da, db in order[1:]:
        slot = da * side + db
        await_block(c, slot, own_sem)
        forward(got.at[c, slot], da, db)
        to_sibling(got.at[c, slot], slot)
        passed.add((da, db))
        advance(1)
    advance(1 << 20)
    out_ref[me] = back[0, c]

    def drain(k, _):
        here = got.at[c, 0]
        pltpu.make_async_remote_copy(
            here, here, send_sem, own_sem.at[0], device_id={"row": me}, device_id_type=MESH
        ).wait_send()
        return 0

    lax.fori_loop(0, 2 * chips - 1, drain, 0)
    whole = out_ref.at[pl.ds(0, rows - 1)]
    done = pltpu.make_async_remote_copy(
        whole, whole, back_sem, ret_sem, device_id={"row": me}, device_id_type=MESH
    )
    done.wait_send()
    done.wait_recv()


def finish(enc_smem, enc_ref, rows_ref, hot_ref, out_ref, buf, mid, lists_a, lists_b):
    nprobe, qcount = enc_ref.shape
    enc = enc_ref[...]

    def gather(j, _):
        def one(q, _):
            at = jnp.maximum(enc_smem[j, q], 0)
            buf[pl.ds(j * qcount + q, 1), :] = rows_ref[pl.ds(at, 1), :]
            return 0

        lax.fori_loop(0, qcount, one, 0, unroll=16)
        return 0

    lax.fori_loop(0, nprobe, gather, 0)
    for j in range(nprobe):
        dst = lists_a if j < SUB else lists_b
        flat = jnp.transpose(buf[j * qcount : (j + 1) * qcount, :])
        flat = jnp.where(enc[j : j + 1, :] < 0, NEG, flat)
        dst[pl.ds(j % SUB, TOPK, stride=SUB), :] = flat
    merge_top_128(lists_a, 0, lists_b, 0, lists_a, 0, mid)
    merge_top_128(lists_a, 0, hot_ref, 0, lists_a, 0, mid)
    for shift in (4, 2, 1):
        merge_top_128(lists_a, 0, lists_a, 0, lists_b, 0, mid, shift)
        lists_a, lists_b = lists_b, lists_a
    out_ref[...] = jnp.transpose(lists_a[pl.ds(0, TOPK, stride=SUB), :])


def shards(queries, probes, hot_lists, cold_lists):
    rows = lax.axis_size("row")
    side = math.isqrt(rows // 2)
    qcount, nprobe = probes.shape
    width = queries.shape[1]
    list_dev, lsize = cold_lists.shape[0], cold_lists.shape[1]
    hot = hot_lists.shape[0]
    cap = 2 * ((qcount * nprobe + list_dev * rows - 1) // (list_dev * rows))
    slots = list_dev * cap
    depth = qcount + slots // 2
    vmem = pl.BlockSpec(memory_space=pltpu.VMEM)
    limit = 60 * 2**20
    f32 = jnp.float32
    column = pltpu.VMEM((lsize * SUB, LANES), f32)
    small = pltpu.VMEM((TOPK * SUB, LANES), f32)

    returned, enc, hot_best = pl.pallas_call(
        functools.partial(exchange, rows, side, cap),
        out_shape=(
            jax.ShapeDtypeStruct((rows, slots, TOPK), f32),
            jax.ShapeDtypeStruct((nprobe, qcount), jnp.int32),
            jax.ShapeDtypeStruct((TOPK * SUB, LANES), f32),
        ),
        in_specs=[vmem] * 4,
        out_specs=(vmem,) * 3,
        scratch_shapes=[
            pltpu.VMEM((depth, width), jnp.bfloat16),
            pltpu.VMEM((slots, rows), f32),
            pltpu.VMEM((qcount, rows * list_dev), f32),
            pltpu.VMEM((2, side * side, depth, width), jnp.bfloat16),
            pltpu.VMEM((list_dev // 2, 2 * LANES, width), f32),
            column,
            column,
            small,
            pltpu.VMEM((side * side, 2, slots, TOPK), f32),
            pltpu.SemaphoreType.DMA,
            pltpu.SemaphoreType.DMA((side * side,)),
            pltpu.SemaphoreType.DMA((side * side,)),
            pltpu.SemaphoreType.DMA,
            pltpu.SemaphoreType.DMA,
        ],
        compiler_params=pltpu.CompilerParams(collective_id=0, has_side_effects=True, vmem_limit_bytes=limit),
    )(probes.T, queries, cold_lists, hot_lists)

    return pl.pallas_call(
        finish,
        out_shape=jax.ShapeDtypeStruct((qcount, TOPK), f32),
        in_specs=[pl.BlockSpec(memory_space=pltpu.SMEM)] + [vmem] * 3,
        out_specs=vmem,
        scratch_shapes=[pltpu.VMEM((nprobe * qcount, TOPK), f32), small, small, small],
        compiler_params=pltpu.CompilerParams(vmem_limit_bytes=limit),
    )(enc, enc, returned.reshape(rows * slots, TOPK), hot_best)


def solution(mesh):
    placed = (
        P(("tenant", "row"), None),
        P(("tenant", "row"), None),
        P("tenant", None, None),
        P(("tenant", "row"), None, None),
    )
    return jax.shard_map(
        shards, mesh=mesh, in_specs=placed, out_specs=P(("tenant", "row"), None), check_vma=False
    )
```

time: 167 us -> 130 us (0.78)
  Pallas kernels: 165 us -> 129 us
    pallas_call x2 -> x1, Pallas kernels: 151 us -> 119 us  [shards(): pl.pallas_call(functools.partial(exchange, rows, side, cap), out_shape=(j...]
    pallas_call x1, Pallas kernels: 14.7 us -> 10.4 us  [shards(): pl.pallas_call(finish, out_shape=jax.ShapeDtypeStruct((qcount, TOPK), f32...]
where the time goes in v2:
time: 130 us; the launch traced here: 129 us
  Pallas kernels  129 us (99%)
    pallas_call x1, Pallas kernels, shards(): pl.pallas_call(functools.partial(exchange, rows, side, cap), out_shape=(j...  119 us
    pallas_call x1, Pallas kernels, shards(): pl.pallas_call(finish, out_shape=jax.ShapeDtypeStruct((qcount, TOPK), f32...  10.4 us

profile of v2, /device:TPU:513, one launch (start us, length us, event | category | flops | bytes accessed | tf_op | source)
XLA Modules:
  0.0 129.5 jit_solution(10591407312172301631)
XLA Ops:
  0.0 119.1 %shard_map.46 = (f32[128,32,128]{2,1,0:T(8,128)}, s32[16,128]{1,0:T(8,128)}, f32[1024,128]{1,0:T(8,128)}) custom-call(s32[16,128]{1,0:T(8,128)} %bitcast.3, bf16[128,256]{1,0:T(8,128)(2,1)} %queries_ref.1, bf16[8,256,256]{2,1,0:T(8,128)(2,1)} %lists_ref.1, bf16[16,256,256]{2,1,0:T(8,128)(2,1)} %hot_ref.1), custom_call_target="tpu_custom_call" | custom-call | tf_op jit(solution)/shard_map/pallas_call | solution.py:422
  119.1 10.4 %shard_map.47 = f32[128,128]{1,0:T(8,128)} custom-call(s32[16,128]{1,0:T(8,128)} %get-tuple-element.8.enc_smem.enc_ref, s32[16,128]{1,0:T(8,128)} %get-tuple-element.8.enc_smem.enc_ref, f32[4096,128]{1,0:T(8,128)} %bitcast.2, f32[1024,128]{1,0:T(8,128)} %get-tuple-element.10.hot_ref), custom_call_target="tpu_custom_call" | custom-call | tf_op jit(solution)/shard_map/pallas_call | solution.py:450

commit v3 on v2

--- a/solution.py
+++ b/solution.py
@@ -10,6 +10,7 @@
 
 MESH = pl.DeviceIdType.MESH
 TOPK = 128
+FIRST = 64
 LANES = 128
 SUB = 8
 NEG = float("-inf")
@@ -49,7 +50,8 @@
 
 
 def row(base, i):
-    return pl.ds(pl.multiple_of((base + i) * SUB, SUB), SUB)
+    at = (base + i) * SUB
+    return pl.ds(at if isinstance(at, int) else pl.multiple_of(at, SUB), SUB)
 
 
 def sort_groups(ref, start, stop, n=32):
@@ -140,8 +142,30 @@
     yield
 
 
-def exchange(rows, side, cap, probes_ref, queries_ref, lists_ref, hot_ref, out_ref, enc_ref, hot_out, block, table, ranks,
-             got, picked, x, y, mid, back, send_sem, own_sem, sib_sem, back_sem, ret_sem):
+def sort_top_64(x, y):
+    sort_groups(x, 0, 4)
+    yield
+    sort_groups(x, 4, 8)
+    yield
+    merge_full_32(x, y, 4)
+    yield
+    for src, dst, count in ((y, x, 2), (x, y, 1)):
+        for g in range(count):
+            for n, inner in enumerate((jnp.maximum, jnp.minimum)):
+                v = half_64(src, g * 128, g * 128 + 64, jnp.maximum, inner)
+                for i in range(32):
+                    dst[row(g * 64 + n * 32, i), :] = v[i]
+        yield
+
+
+def run(pieces):
+    for _ in pieces:
+        pass
+
+
+def exchange(rows, side, cap, probes_ref, queries_ref, lists_ref, hot_ref, best_ref, flag_ref, block, table, ranks,
+             got, picked, x, y, mid, back, out_ref, enc_ref, line_ref, enc_smem, hot_out, buf, lists_a, lists_b, note, notes_x, notes_y,
+             send_sem, own_sem, sib_sem, back_sem, ret_sem, enc_sem, note_sem, nx_sem, ny_sem):
     me = lax.axis_index("row")
     mx, my, c = me // (2 * side), (me // 2) % side, me % 2
     chips = side * side
@@ -254,9 +278,14 @@
         for j in range(nprobe):
             p = probes[:, j : j + 1]
             mine = jnp.sum(jnp.where(p == ids, ranks[...], 0.0), axis=1, keepdims=True)
-            code = jnp.where(p < hot, -1.0 - p, (p - hot) * cap + mine)
+            n = p.astype(jnp.int32) - hot
+            own = n % list_dev
+            line = (n // list_dev) * (slots // 2) + (own // 4) * SUB + (own % 2) * cap
+            code = jnp.where(n < 0, -1.0, ((line * 2) + (own // 2) % 2).astype(f32) + 2.0 * mine)
             enc = jnp.where(columns == j, code, enc)
-        enc_ref[...] = jnp.transpose(enc)[0:nprobe, :].astype(jnp.int32)
+        codes = jnp.transpose(enc)[0:nprobe, :].astype(jnp.int32)
+        enc_ref[...] = codes
+        line_ref[...] = jnp.clip(codes >> 1, 0, out_ref.shape[0] - 1)
         yield
 
     def hot_work():
@@ -278,6 +307,7 @@
     def batch(b):
         mine = order[b * per : (b + 1) * per]
         for k0 in range(0, per, step):
+            yield set(mine[k0 : k0 + step])
             some = [(k, t) for k in range(k0, k0 + step) for t in range(2)]
             for t in range(2):
 
@@ -297,7 +327,7 @@
                 for m in range(pairs):
                     low = t * LANES + k * SUB
                     picked[m, low : low + SUB, :] = chosen[m * SUB : (m + 1) * SUB, :]
-            yield
+        yield
         for m in range(pairs):
             right = picked[m].astype(bf16)
             even_s = lax.dot_general(lists_ref[2 * m], right, last, preferred_element_type=f32)
@@ -306,11 +336,12 @@
             for t in range(2):
                 x[pl.ds(2 * m + t, lsize, stride=SUB), :] = s[:, t * LANES : (t + 1) * LANES]
             yield
-        yield from sort_top_128(x, y, mid)
-        for m in range(pairs):
+        yield from sort_top_64(x, y)
+        for m in range(pairs // 2):
             for t in range(2):
-                sorted_rows = jnp.transpose(y[pl.ds(2 * m + t, TOPK, stride=SUB), :])
-                back[b * per : (b + 1) * per, t, m * SUB : (m + 1) * SUB, :] = sorted_rows.reshape(per, SUB, TOPK)
+                two = [y[pl.ds(2 * (2 * m + n) + t, FIRST, stride=SUB), :] for n in range(2)]
+                sorted_rows = jnp.transpose(jnp.concatenate(two, axis=0))
+                back[b * per : (b + 1) * per, t, m * SUB : (m + 1) * SUB, :] = sorted_rows.reshape(per, SUB, LANES)
         yield
         for k in range(per):
             dx, dy = mine[k]
@@ -318,7 +349,7 @@
 
                 def give():
                     pltpu.make_async_remote_copy(
-                        back.at[b * per + k, t], out_ref.at[me], back_sem, ret_sem,
+                        back.at[b * per + k, t], home, back_sem, ret_sem,
                         device_id={"row": at(dx, dy, t)}, device_id_type=MESH,
                     ).start()
 
@@ -331,24 +362,22 @@
 
     forward(block, 0, 0)
     to_sibling(block, 0)
-
-    todo = [positions(), hot_work()]
-    batches = [(set(order[b * per : (b + 1) * per]), batch(b)) for b in range(chips // per)]
+    home = out_ref.at[pl.ds(pl.multiple_of(me * (slots // 2), SUB), slots // 2)]
+
+    todo = [positions(), hot_work()] + [batch(b) for b in range(chips // per)]
     passed = {(0, 0)}
+    need = [None]
 
     def advance(count):
-        while count and (todo or batches):
-            if not todo:
-                need, work = batches[0]
-                if not all((a, b) in passed and (b, a) in passed for a, b in need):
-                    return
-                batches.pop(0)
-                todo.append(work)
+        while count and todo:
+            if need[0] and not all((a, b) in passed and (b, a) in passed for a, b in need[0]):
+                return
             try:
-                next(todo[0])
+                need[0] = next(todo[0])
                 count -= 1
             except StopIteration:
                 todo.pop(0)
+                need[0] = None
 
     for da, db in order[1:]:
         slot = da * side + db
@@ -358,6 +387,260 @@
         passed.add((da, db))
         advance(1)
     advance(1 << 20)
+    home[...] = back[0, c]
+
+    def drain(k, _):
+        here = got.at[c, 0]
+        pltpu.make_async_remote_copy(
+            here, here, send_sem, own_sem.at[0], device_id={"row": me}, device_id_type=MESH
+        ).wait_send()
+        return 0
+
+    lax.fori_loop(0, 2 * chips - 1, drain, 0)
+    to_smem = pltpu.make_async_copy(line_ref, enc_smem, enc_sem)
+    to_smem.start()
+    to_smem.wait()
+    whole = out_ref.at[pl.ds(0, (rows - 1) * (slots // 2))]
+    done = pltpu.make_async_remote_copy(
+        whole, whole, back_sem, ret_sem, device_id={"row": me}, device_id_type=MESH
+    )
+    done.wait_send()
+    done.wait_recv()
+
+    assert out_ref.shape[0] & (out_ref.shape[0] - 1) == 0
+
+    def gather(j, _):
+        def one(q, _):
+            line = enc_smem[j, q] & (out_ref.shape[0] - 1)
+            buf[pl.ds(j * qcount + q, 1), :] = out_ref[pl.ds(line, 1), :]
+            return 0
+
+        lax.fori_loop(0, qcount, one, 0, unroll=16)
+        return 0
+
+    lax.fori_loop(0, nprobe, gather, 0)
+    enc = enc_ref[...]
+    for j in range(nprobe):
+        both = jnp.transpose(buf[j * qcount : (j + 1) * qcount, :])
+        flat = jnp.where(enc[j : j + 1, :] % 2 == 0, both[0:FIRST, :], both[FIRST : 2 * FIRST, :])
+        flat = jnp.where(enc[j : j + 1, :] < 0, NEG, flat)
+        lists_a[pl.ds((j // SUB) * FIRST * SUB + j % SUB, FIRST, stride=SUB), :] = flat
+
+    least = jnp.maximum(lists_a[row(FIRST - 1, 0), :], lists_a[row(2 * FIRST - 1, 0), :])
+    for shift in (4, 2, 1):
+        least = jnp.maximum(least, pltpu.roll(least, shift, 0))
+    count = jnp.zeros((SUB, LANES), f32)
+    for k in range(TOPK):
+        count += (lists_a[row(k, 0), :] >= least).astype(f32) + (hot_out[row(k, 0), :] >= least).astype(f32)
+    for shift in (4, 2, 1):
+        count += pltpu.roll(count, shift, 0)
+    note[0] = (count < float(TOPK)).astype(f32)
+    merge_full_64(lists_a, lists_b, 1)
+
+    def tell(number, src, dx, dy, core, dst, sem):
+        pltpu.make_async_remote_copy(
+            src, dst.at[number], note_sem, sem, device_id={"row": at(dx, dy, core)}, device_id_type=MESH
+        ).start()
+
+    def heard(dst, sem):
+        pltpu.make_async_remote_copy(dst, dst, note_sem, sem, device_id={"row": me}, device_id_type=MESH).wait_recv()
+
+    near = [(dx, t) for dx in range(side) for t in range(2)]
+    for dx, t in near[1:]:
+        tell(2 * dx + t - 1, note.at[0], dx, 0, (c + t) % 2, notes_x, nx_sem)
+    merge_top_128(lists_b, 0, hot_out, 0, lists_a, 0, mid)
+    merge_top_128(lists_a, 0, lists_a, 0, lists_b, 0, mid, 4)
+    heard(notes_x, nx_sem)
+    note[1] = jnp.maximum(note[0], jnp.max(notes_x[...], axis=0))
+    merge_top_128(lists_b, 0, lists_b, 0, lists_a, 0, mid, 2)
+    for dy in range(1, side):
+        tell(dy - 1, note.at[1], 0, dy, c, notes_y, ny_sem)
+    merge_top_128(lists_a, 0, lists_a, 0, lists_b, 0, mid, 1)
+    best_ref[...] = jnp.transpose(lists_b[pl.ds(0, TOPK, stride=SUB), :])
+    heard(notes_y, ny_sem)
+    flag_ref[0, 0] = jnp.max(jnp.maximum(note[1], jnp.max(notes_y[...], axis=0))).astype(jnp.int32)
+    for sent in (notes_x, notes_y):
+        pltpu.make_async_remote_copy(
+            sent, sent, note_sem, nx_sem, device_id={"row": me}, device_id_type=MESH
+        ).wait_send()
+
+
+def slow_prepare(rows, list_dev, hot, cap, probes_ref, queries_ref, block_ref, enc_ref, table):
+    qcount, nprobe = probes_ref.shape
+    cold = rows * list_dev
+    lane = lax.broadcasted_iota(jnp.int32, (qcount, cold), 1)
+    ids = (lane % rows) * list_dev + lane // rows + hot
+    probes = probes_ref[...]
+    named = jnp.zeros((qcount, cold), jnp.float32)
+    for j in range(nprobe):
+        named = jnp.where(probes[:, j : j + 1] == ids, 1.0, named)
+    below = lax.broadcasted_iota(jnp.int32, (qcount, qcount), 1) < lax.broadcasted_iota(
+        jnp.int32, (qcount, qcount), 0
+    )
+    rank = jnp.dot(
+        below.astype(jnp.float32).astype(jnp.bfloat16),
+        named.astype(jnp.bfloat16),
+        preferred_element_type=jnp.float32,
+    )
+    number = lax.broadcasted_iota(jnp.int32, (qcount, cold), 0).astype(jnp.float32) + 1.0
+    for r in range(cap):
+        held = jnp.where((named > 0) & (rank == float(r)), number, 0.0)
+        line = jnp.sum(held, axis=0, keepdims=True)
+        for l in range(list_dev):
+            e = l * cap + r
+            table[e : e + 1, :] = line[:, l * rows : (l + 1) * rows]
+    half = list_dev * cap // 2
+    block_ref[0:qcount, :] = queries_ref[...]
+    block_ref[qcount : qcount + half, 0:rows] = table[0:half, :].astype(jnp.bfloat16)
+    block_ref[qcount : qcount + half, rows : 2 * rows] = table[half : 2 * half, :].astype(
+        jnp.bfloat16
+    )
+    columns = lax.broadcasted_iota(jnp.int32, (qcount, LANES), 1)
+    enc = jnp.zeros((qcount, LANES), jnp.float32)
+    for j in range(nprobe):
+        p = probes[:, j : j + 1]
+        mine = jnp.sum(jnp.where(p == ids, rank, 0.0), axis=1, keepdims=True)
+        pf = p.astype(jnp.float32)
+        code = jnp.where(p < hot, -1.0 - pf, (pf - hot) * cap + mine)
+        enc = jnp.where(columns == j, code, enc)
+    enc_ref[...] = jnp.transpose(enc)[0:nprobe, :].astype(jnp.int32)
+
+
+def slow_exchange(rows, side, list_dev, cap, block_ref, lists_ref, out_ref, got, picked, x, y, mid, back,
+             send_sem, own_sem, sib_sem, back_sem, ret_sem):
+    me = lax.axis_index("row")
+    mx, my, c = me // (2 * side), (me // 2) % side, me % 2
+    chips = side * side
+    depth = block_ref.shape[0]
+    half = list_dev * cap // 2
+    qcount = depth - half
+    slots = list_dev * cap
+    pairs = list_dev // 2
+
+    def at(dx, dy, core):
+        return (((mx + dx) % side) * side + (my + dy) % side) * 2 + core
+
+    barrier = pltpu.get_barrier_semaphore()
+
+    def greet(k, _):
+        pl.semaphore_signal(barrier, 1, device_id={"row": (me + k) % rows}, device_id_type=MESH)
+        return 0
+
+    lax.fori_loop(1, rows, greet, 0)
+    pl.semaphore_wait(barrier, rows - 1)
+
+    def along(da, db):
+        return at(da * (1 - c) + db * c, da * c + db * (1 - c), c)
+
+    def push(src, da, db, to_a, to_b):
+        slot = ((da - to_a) % side) * side + (db - to_b) % side
+        pltpu.make_async_remote_copy(
+            src, got.at[c, slot], send_sem, own_sem.at[slot],
+            device_id={"row": along(to_a % side, to_b % side)}, device_id_type=MESH,
+        ).start()
+
+    def signed(d):
+        return d if d <= side // 2 else d - side
+
+    def forward(src, da, db):
+        sa, sb = signed(da), signed(db)
+        far = side // 2
+        if db == 0:
+            if sa <= 0 and -sa + 1 <= far and da != far:
+                push(src, da, db, 1, 0)
+            if sa >= 0 and sa + 1 <= far - 1:
+                push(src, da, db, -1, 0)
+        plus, minus = (far, far - 1) if da % 2 == 0 else (far - 1, far)
+        came_plus = db == 0 or sb < 0
+        came_minus = db == 0 or (sb > 0 and db != far)
+        if came_plus and (0 if db == 0 else -sb) + 1 <= plus:
+            push(src, da, db, 0, 1)
+        if came_minus and (0 if db == 0 else sb) + 1 <= minus:
+            push(src, da, db, 0, -1)
+
+    def to_sibling(src, slot):
+        pltpu.make_async_remote_copy(
+            src, got.at[c, slot], send_sem, sib_sem.at[slot],
+            device_id={"row": at(0, 0, 1 - c)}, device_id_type=MESH,
+        ).start()
+
+    forward(block_ref, 0, 0)
+    to_sibling(block_ref, 0)
+    got[c, 0] = block_ref[...]
+    order = [(a, b) for a in range(side) for b in range(side) if (a, b) != (0, 0)]
+    order.sort(key=lambda o: (abs(signed(o[0])) + abs(signed(o[1])), abs(signed(o[1])), o))
+    for da, db in order:
+        slot = da * side + db
+        here = got.at[c, slot]
+        pltpu.make_async_remote_copy(
+            here, here, send_sem, own_sem.at[slot], device_id={"row": me}, device_id_type=MESH
+        ).wait_recv()
+        forward(here, da, db)
+        to_sibling(here, slot)
+
+    share = chips // (LANES // SUB)
+    per = chips // share
+    choose = (lax.broadcasted_iota(jnp.int32, (rows, LANES), 0) == me).astype(jnp.float32).astype(jnp.bfloat16)
+    number = lax.broadcasted_iota(jnp.int32, (slots, qcount), 1).astype(jnp.float32) + 1.0
+    odd = (lax.broadcasted_iota(jnp.int32, (lists_ref.shape[1], 2 * LANES), 1) // cap) % 2 == 1
+
+    def batch(b, _):
+        def take(k, _):
+            i = b * per + k
+            for t in range(2):
+                slot = i if t == 0 else (i % side) * side + i // side
+                here = got.at[t, slot]
+
+                @pl.when((c != t))
+                def _():
+                    pltpu.make_async_remote_copy(
+                        here, here, send_sem, sib_sem.at[slot], device_id={"row": me}, device_id_type=MESH
+                    ).wait_recv()
+
+                table = jnp.concatenate(
+                    [got[t, slot, qcount:depth, 0:rows], got[t, slot, qcount:depth, rows : 2 * rows]], axis=0
+                )
+                wide = jnp.dot(table, choose, preferred_element_type=jnp.float32)
+                hits = (wide == number).astype(jnp.float32).astype(jnp.bfloat16)
+                chosen = jnp.dot(hits, got[t, slot, 0:qcount, :], preferred_element_type=jnp.float32)
+                for m in range(pairs):
+                    picked[m, pl.ds(pl.multiple_of(t * LANES + k * SUB, SUB), SUB), :] = chosen[
+                        m * SUB : (m + 1) * SUB, :
+                    ]
+            return 0
+
+        lax.fori_loop(0, per, take, 0)
+
+        for m in range(pairs):
+            right = picked[m].astype(jnp.bfloat16)
+            dims = (((1,), (1,)), ((), ()))
+            even_s = lax.dot_general(lists_ref[2 * m], right, dims, preferred_element_type=jnp.float32)
+            odd_s = lax.dot_general(lists_ref[2 * m + 1], right, dims, preferred_element_type=jnp.float32)
+            s = jnp.where(odd, odd_s, even_s)
+            for t in range(2):
+                x[pl.ds(2 * m + t, s.shape[0], stride=SUB), :] = s[:, t * LANES : (t + 1) * LANES]
+        run(sort_top_128(x, y, mid))
+        for m in range(pairs):
+            for t in range(2):
+                sorted_rows = jnp.transpose(y[pl.ds(2 * m + t, TOPK, stride=SUB), :])
+                back[pl.ds(b * per, per), t, m * SUB : (m + 1) * SUB, :] = sorted_rows.reshape(per, SUB, TOPK)
+
+        def give(k, _):
+            i = b * per + k
+            for t in range(2):
+
+                @pl.when((i != 0) | (c != t))
+                def _():
+                    pltpu.make_async_remote_copy(
+                        back.at[i, t], out_ref.at[me], back_sem, ret_sem,
+                        device_id={"row": at(i // side, i % side, t)}, device_id_type=MESH,
+                    ).start()
+            return 0
+
+        lax.fori_loop(0, per, give, 0)
+        return 0
+
+    lax.fori_loop(0, share, batch, 0)
     out_ref[me] = back[0, c]
 
     def drain(k, _):
@@ -376,8 +659,9 @@
     done.wait_recv()
 
 
-def finish(enc_smem, enc_ref, rows_ref, hot_ref, out_ref, buf, mid, lists_a, lists_b):
+def slow_finish(enc_smem, enc_ref, rows_ref, queries_ref, hot_ref, out_ref, buf, x, y, mid, lists_a, lists_b):
     nprobe, qcount = enc_ref.shape
+    hot = hot_ref.shape[0]
     enc = enc_ref[...]
 
     def gather(j, _):
@@ -396,7 +680,16 @@
         flat = jnp.where(enc[j : j + 1, :] < 0, NEG, flat)
         dst[pl.ds(j % SUB, TOPK, stride=SUB), :] = flat
     merge_top_128(lists_a, 0, lists_b, 0, lists_a, 0, mid)
-    merge_top_128(lists_a, 0, hot_ref, 0, lists_a, 0, mid)
+    for g in range(hot // SUB):
+        for s in range(SUB):
+            h = g * SUB + s
+            scores = lax.dot_general(
+                hot_ref[h], queries_ref[...], (((1,), (1,)), ((), ())), preferred_element_type=jnp.float32
+            )
+            asked = jnp.max((enc == -1 - h).astype(jnp.float32), axis=0, keepdims=True)
+            x[pl.ds(s, scores.shape[0], stride=SUB), :] = jnp.where(asked > 0, scores, NEG)
+        run(sort_top_128(x, y, mid))
+        merge_top_128(lists_a, 0, y, 0, lists_a, 0, mid)
     for shift in (4, 2, 1):
         merge_top_128(lists_a, 0, lists_a, 0, lists_b, 0, mid, shift)
         lists_a, lists_b = lists_b, lists_a
@@ -419,15 +712,14 @@
     column = pltpu.VMEM((lsize * SUB, LANES), f32)
     small = pltpu.VMEM((TOPK * SUB, LANES), f32)
 
-    returned, enc, hot_best = pl.pallas_call(
+    best, flag = pl.pallas_call(
         functools.partial(exchange, rows, side, cap),
         out_shape=(
-            jax.ShapeDtypeStruct((rows, slots, TOPK), f32),
-            jax.ShapeDtypeStruct((nprobe, qcount), jnp.int32),
-            jax.ShapeDtypeStruct((TOPK * SUB, LANES), f32),
+            jax.ShapeDtypeStruct((qcount, TOPK), f32),
+            jax.ShapeDtypeStruct((1, 1), jnp.int32),
         ),
         in_specs=[vmem] * 4,
-        out_specs=(vmem,) * 3,
+        out_specs=(vmem, pl.BlockSpec(memory_space=pltpu.SMEM)),
         scratch_shapes=[
             pltpu.VMEM((depth, width), jnp.bfloat16),
             pltpu.VMEM((slots, rows), f32),
@@ -437,24 +729,75 @@
             column,
             column,
             small,
-            pltpu.VMEM((side * side, 2, slots, TOPK), f32),
+            pltpu.VMEM((side * side, 2, slots // 2, LANES), f32),
+            pltpu.VMEM((rows * slots // 2, LANES), f32),
+            pltpu.VMEM((nprobe, qcount), jnp.int32),
+            pltpu.VMEM((nprobe, qcount), jnp.int32),
+            pltpu.SMEM((nprobe, qcount), jnp.int32),
+            small,
+            pltpu.VMEM((nprobe * qcount, LANES), f32),
+            small,
+            small,
+            pltpu.VMEM((2, SUB, LANES), f32),
+            pltpu.VMEM((2 * side - 1, SUB, LANES), f32),
+            pltpu.VMEM((side - 1, SUB, LANES), f32),
             pltpu.SemaphoreType.DMA,
             pltpu.SemaphoreType.DMA((side * side,)),
             pltpu.SemaphoreType.DMA((side * side,)),
             pltpu.SemaphoreType.DMA,
             pltpu.SemaphoreType.DMA,
+            pltpu.SemaphoreType.DMA,
+            pltpu.SemaphoreType.DMA,
+            pltpu.SemaphoreType.DMA,
+            pltpu.SemaphoreType.DMA,
         ],
         compiler_params=pltpu.CompilerParams(collective_id=0, has_side_effects=True, vmem_limit_bytes=limit),
     )(probes.T, queries, cold_lists, hot_lists)
 
-    return pl.pallas_call(
-        finish,
-        out_shape=jax.ShapeDtypeStruct((qcount, TOPK), f32),
-        in_specs=[pl.BlockSpec(memory_space=pltpu.SMEM)] + [vmem] * 3,
-        out_specs=vmem,
-        scratch_shapes=[pltpu.VMEM((nprobe * qcount, TOPK), f32), small, small, small],
-        compiler_params=pltpu.CompilerParams(vmem_limit_bytes=limit),
-    )(enc, enc, returned.reshape(rows * slots, TOPK), hot_best)
+    def full(best, queries, probes, hot_lists, cold_lists):
+        block, enc = pl.pallas_call(
+            functools.partial(slow_prepare, rows, list_dev, hot, cap),
+            out_shape=(
+                jax.ShapeDtypeStruct((depth, width), jnp.bfloat16),
+                jax.ShapeDtypeStruct((nprobe, qcount), jnp.int32),
+            ),
+            in_specs=[vmem] * 2,
+            out_specs=(vmem, vmem),
+            scratch_shapes=[pltpu.VMEM((slots, rows), f32)],
+            compiler_params=pltpu.CompilerParams(vmem_limit_bytes=limit),
+        )(probes, queries)
+        returned = pl.pallas_call(
+            functools.partial(slow_exchange, rows, side, list_dev, cap),
+            out_shape=jax.ShapeDtypeStruct((rows, slots, TOPK), f32),
+            in_specs=[vmem] * 2,
+            out_specs=vmem,
+            scratch_shapes=[
+                pltpu.VMEM((2, side * side, depth, width), jnp.bfloat16),
+                pltpu.VMEM((list_dev // 2, 2 * LANES, width), f32),
+                column,
+                column,
+                small,
+                pltpu.VMEM((side * side, 2, slots, TOPK), f32),
+                pltpu.SemaphoreType.DMA,
+                pltpu.SemaphoreType.DMA((side * side,)),
+                pltpu.SemaphoreType.DMA((side * side,)),
+                pltpu.SemaphoreType.DMA,
+                pltpu.SemaphoreType.DMA,
+            ],
+            compiler_params=pltpu.CompilerParams(collective_id=1, has_side_effects=True, vmem_limit_bytes=limit),
+        )(block, cold_lists)
+        return pl.pallas_call(
+            slow_finish,
+            out_shape=jax.ShapeDtypeStruct((qcount, TOPK), f32),
+            in_specs=[pl.BlockSpec(memory_space=pltpu.SMEM)] + [vmem] * 4,
+            out_specs=vmem,
+            scratch_shapes=[pltpu.VMEM((nprobe * qcount, TOPK), f32), column, column, small, small, small],
+            compiler_params=pltpu.CompilerParams(vmem_limit_bytes=limit),
+        )(enc, enc, returned.reshape(rows * slots, TOPK), queries, hot_lists)
+
+    return lax.cond(
+        flag[0, 0] > 0, full, lambda best, *_: best, best, queries, probes, hot_lists, cold_lists
+    )
 
 
 def solution(mesh):

time: 130 us -> 107 us (0.82)
  Pallas kernels: 129 us -> 106 us
    pallas_call x1, Pallas kernels: 119 us -> 106 us  [shards(): pl.pallas_call(functools.partial(exchange, rows, side, cap), out_shape=(j...]
    pallas_call x1 -> x0, Pallas kernels: 10.4 us -> none  [shards(): pl.pallas_call(finish, out_shape=jax.ShapeDtypeStruct((qcount, TOPK), f32...]
where the time goes in v3:
time: 107 us
  Pallas kernels  106 us (99%)
    pallas_call x1, Pallas kernels, shards(): pl.pallas_call(functools.partial(exchange, rows, side, cap), out_shape=(j...  106 us

profile of v3, /device:TPU:513, one launch (start us, length us, event | category | flops | bytes accessed | tf_op | source)
XLA Modules:
  0.0 107.4 jit_solution(496609037315775061)
XLA Ops:
  0.0 0.0 copy-start.1
  0.0 0.0 copy-start
  0.0 0.0 copy-start.3
  0.0 0.0 copy-start.2
  0.0 105.9 %shard_map.48 = (f32[128,128]{1,0:T(8,128)S(1)}, s32[1,1]{1,0:T(1,128)}) custom-call(s32[16,128]{1,0:T(8,128)} %bitcast.4, bf16[128,256]{1,0:T(8,128)(2,1)} %queries_ref.1, bf16[8,256,256]{2,1,0:T(8,128)(2,1)} %lists_ref.1, bf16[16,256,256]{2,1,0:T(8,128)(2,1)} %hot_ref.1), custom_call_target="tpu_custom_call" | custom-call | tf_op jit(solution)/shard_map/pallas_call | solution.py:715
  106.5 0.0 copy-done.1
  106.5 0.0 copy-done
  106.5 0.0 copy-done.3
  106.5 0.0 copy-done.2
  106.5 0.2 conditional.1
  106.8 0.6 copy.11
Async XLA Ops:
  0.0 106.5 %copy-start.1 = (bf16[8,256,256]{2,1,0:T(8,128)(2,1)S(1)}, bf16[8,256,256]{2,1,0:T(8,128)(2,1)}, u32[]{:S(2)}) copy-start(bf16[8,256,256]{2,1,0:T(8,128)(2,1)} %lists_ref.1) | copy-start | bytes 3145732
  0.0 106.5 %copy-start = (bf16[16,256,256]{2,1,0:T(8,128)(2,1)S(1)}, bf16[16,256,256]{2,1,0:T(8,128)(2,1)}, u32[]{:S(2)}) copy-start(bf16[16,256,256]{2,1,0:T(8,128)(2,1)} %hot_ref.1) | copy-start | bytes 6291460
  0.0 106.5 %copy-start.3 = (s32[128,16]{0,1:T(8,128)S(1)}, s32[128,16]{0,1:T(8,128)}, u32[]{:S(2)}) copy-start(s32[128,16]{0,1:T(8,128)} %param.7) | copy-start | bytes 24580
  0.0 106.5 %copy-start.2 = (bf16[128,256]{1,0:T(8,128)(2,1)S(1)}, bf16[128,256]{1,0:T(8,128)(2,1)}, u32[]{:S(2)}) copy-start(bf16[128,256]{1,0:T(8,128)(2,1)} %queries_ref.1) | copy-start | bytes 196612

commit v4 on v3

--- a/solution.py
+++ b/solution.py
@@ -385,7 +385,7 @@
         forward(got.at[c, slot], da, db)
         to_sibling(got.at[c, slot], slot)
         passed.add((da, db))
-        advance(1)
+        advance(1 if len(passed) < 14 else 2)
     advance(1 << 20)
     home[...] = back[0, c]
 

time: 107 us -> 110 us (1.028)
  Pallas kernels: 106 us -> 108 us
    pallas_call x1, Pallas kernels: 106 us -> 108 us  [shards(): pl.pallas_call(functools.partial(exchange, rows, side, cap), out_shape=(j...]
where the time goes in v4:
time: 110 us; the launch traced here: 109 us
  Pallas kernels  108 us (98%)
    pallas_call x1, Pallas kernels, shards(): pl.pallas_call(functools.partial(exchange, rows, side, cap), out_shape=(j...  108 us

profile of v4, /device:TPU:513, one launch (start us, length us, event | category | flops | bytes accessed | tf_op | source)
XLA Modules:
  0.0 109.4 jit_solution(2147760588444930653)
XLA Ops:
  0.0 0.0 copy-start.1
  0.0 0.0 copy-start
  0.0 0.0 copy-start.3
  0.0 0.0 copy-start.2
  0.0 107.9 %shard_map.48 = (f32[128,128]{1,0:T(8,128)S(1)}, s32[1,1]{1,0:T(1,128)}) custom-call(s32[16,128]{1,0:T(8,128)} %bitcast.4, bf16[128,256]{1,0:T(8,128)(2,1)} %queries_ref.1, bf16[8,256,256]{2,1,0:T(8,128)(2,1)} %lists_ref.1, bf16[16,256,256]{2,1,0:T(8,128)(2,1)} %hot_ref.1), custom_call_target="tpu_custom_call" | custom-call | tf_op jit(solution)/shard_map/pallas_call | solution.py:715
  108.5 0.0 copy-done.1
  108.5 0.0 copy-done
  108.5 0.0 copy-done.3
  108.5 0.0 copy-done.2
  108.5 0.2 conditional.1
  108.8 0.6 copy.11
Async XLA Ops:
  0.0 108.5 %copy-start.1 = (bf16[8,256,256]{2,1,0:T(8,128)(2,1)S(1)}, bf16[8,256,256]{2,1,0:T(8,128)(2,1)}, u32[]{:S(2)}) copy-start(bf16[8,256,256]{2,1,0:T(8,128)(2,1)} %lists_ref.1) | copy-start | bytes 3145732
  0.0 108.5 %copy-start = (bf16[16,256,256]{2,1,0:T(8,128)(2,1)S(1)}, bf16[16,256,256]{2,1,0:T(8,128)(2,1)}, u32[]{:S(2)}) copy-start(bf16[16,256,256]{2,1,0:T(8,128)(2,1)} %hot_ref.1) | copy-start | bytes 6291460
  0.0 108.5 %copy-start.3 = (s32[128,16]{0,1:T(8,128)S(1)}, s32[128,16]{0,1:T(8,128)}, u32[]{:S(2)}) copy-start(s32[128,16]{0,1:T(8,128)} %param.7) | copy-start | bytes 24580
  0.0 108.5 %copy-start.2 = (bf16[128,256]{1,0:T(8,128)(2,1)S(1)}, bf16[128,256]{1,0:T(8,128)(2,1)}, u32[]{:S(2)}) copy-start(bf16[128,256]{1,0:T(8,128)(2,1)} %queries_ref.1) | copy-start | bytes 196612
